TPU v7x, 32 devices: a whole 2x2x4 slice. The times are simulated.
32 devices in a mesh: rep: 4 (over y, x), ep: 8 (over z, core).
Axes of the slice: x: 2, y: 2, z: 4, core: 2. Of those that a mesh axis runs over, the one named last changes fastest.
Arguments:
- hidden: bfloat16 [4, 1024, 2, 2048], P(None, ('rep', 'ep')), may hold values from -6 to 6
- out_grad: bfloat16 [4, 1024, 7168], P(None, ('rep', 'ep')), may hold values from -0.375 to 0.375
- route_weight: float32 [4, 1024, 2], P(None, ('rep', 'ep')), may hold values from 0.05 to 1
- expert_ids: int32 [4, 1024, 2], P(None, ('rep', 'ep')), may hold values from 0 to 7, as said below
Outputs:
- grad_down: bfloat16 [8, 2048, 7168], P('ep', None, 'rep')
- expert_load: float32 [8], replicated
Inputs may be any that keep to these rules, and one draw needn't show every extreme that they name: `expert_ids`: in each micro-batch the 32 tokens of one device (aligned blocks of 32 tokens) name no expert in more than 16 pairs, and some expert is named in exactly 16; the 2 experts of a token differ.
All inputs are finite; a program needn't handle non-finite values.
Results may differ from a plain program's by a relative error of at most 0.0049.
Values may be sent and summed in bfloat16 or wider, within the bound.
A program may use at most 192 MiB of HBM per device.

v0:
```python
import jax
import jax.numpy as jnp
from jax import lax
from jax.sharding import PartitionSpec as P


def body(hidden, out_grad, route_weight, expert_ids):
    micro_count, tokens_here, choices_per, hidden_width = hidden.shape
    model_width = out_grad.shape[2]
    replicas = lax.axis_size("rep")
    owners = lax.axis_size("ep")
    capacity = 2 * tokens_here * choices_per // owners
    column_width = model_width // replicas
    pair_count = tokens_here * choices_per
    slot_rows = owners * capacity
    slot_index = jnp.arange(slot_rows, dtype=jnp.int32)
    expert_index = jnp.arange(owners, dtype=jnp.int32)
    pair_loads = jnp.zeros((owners,), jnp.float32)
    contract_rows = (((0,), (0,)), ((), ()))
    hidden_stack = []
    grad_stack = []
    for micro_step in range(micro_count):
        route_ids = expert_ids[micro_step].reshape(pair_count)
        matches = (route_ids[:, None] == expert_index[None, :]).astype(jnp.int32)
        earlier = jnp.cumsum(matches, axis=0) - matches
        position = jnp.sum(earlier * matches, axis=1)
        slot_of_pair = route_ids * capacity + position
        selector = (slot_index[:, None] == slot_of_pair[None, :]).astype(jnp.bfloat16)
        pair_loads = pair_loads + jnp.sum(matches, axis=0).astype(jnp.float32)
        scaled = (
            route_weight[micro_step][:, :, None]
            * out_grad[micro_step][:, None, :].astype(jnp.float32)
        ).astype(jnp.bfloat16)
        scaled = scaled.reshape(pair_count, model_width)
        pair_hidden = hidden[micro_step].reshape(pair_count, hidden_width)
        send_hidden = jnp.dot(selector, pair_hidden, preferred_element_type=jnp.float32).astype(
            jnp.bfloat16
        )
        send_grad = jnp.dot(selector, scaled, preferred_element_type=jnp.float32).astype(
            jnp.bfloat16
        )
        owner_hidden, owner_grad = (
            lax.all_to_all(
                send_hidden.reshape(owners, capacity, hidden_width),
                "ep",
                split_axis=0,
                concat_axis=0,
                tiled=True,
            ),
            lax.all_to_all(
                send_grad.reshape(owners, capacity, model_width),
                "ep",
                split_axis=0,
                concat_axis=0,
                tiled=True,
            ),
        )
        hidden_stack.append(owner_hidden.reshape(slot_rows, hidden_width))
        grad_stack.append(owner_grad.reshape(slot_rows, model_width))
    all_rows = micro_count * slot_rows
    stacked_hidden = jnp.concatenate(hidden_stack, axis=0).reshape(1, all_rows, hidden_width)
    stacked_grad = jnp.concatenate(grad_stack, axis=0).reshape(1, all_rows, model_width)
    grad_blocks = lax.all_to_all(stacked_grad, "rep", split_axis=2, concat_axis=0, tiled=True)
    flat_grad = grad_blocks.reshape(replicas * all_rows, column_width)
    gradient = lax.dot_general(
        lax.all_gather(stacked_hidden.reshape(all_rows, hidden_width), "rep", axis=0, tiled=True),
        flat_grad,
        contract_rows,
        preferred_element_type=jnp.float32,
    )
    all_loads = lax.psum(pair_loads, ("rep", "ep"))
    expert_load = all_loads / float(micro_count * tokens_here * replicas * choices_per)
    return (gradient.astype(jnp.bfloat16).reshape(1, hidden_width, column_width), expert_load)


def solution(mesh):
    return jax.shard_map(
        body,
        mesh=mesh,
        in_specs=(
            P(None, ("rep", "ep"), None, None),
            P(None, ("rep", "ep"), None),
            P(None, ("rep", "ep"), None),
            P(None, ("rep", "ep"), None),
        ),
        out_specs=(P("ep", None, "rep"), P()),
        check_vma=False,
    )
```

profile of v0, /device:TPU:3, one launch (start us, length us, event | category | flops | bytes accessed | tf_op | source)
XLA Modules:
  0.0 551.9 jit_solution(14547247014359509519)
XLA Ops:
  7.2 0.7 fusion.23
  8.0 0.1 reshape_squeeze.24
  8.3 0.1 reshape_squeeze.26
  8.4 0.1 reduce_window_sum.22
  8.6 0.2 fusion.17
  8.8 2.2 fusion.21
  11.0 0.1 reshape_squeeze.25
  11.2 1.1 convolution_convert_fusion.8
  12.2 5.5 %all-to-all-start = ((bf16[8,16,2048]{2,1,0:T(8,128)(2,1)}), bf16[8,16,2048]{2,1,0:T(8,128)(2,1)S(1)}, u32[]{:S(2)}, u32[]{:S(2)}) async-start(bf16[8,16,2048]{2,1,0:T(8,128)(2,1)} %bitcast), calls=%async_computation | async-start | bytes 1048576 | tf_op jit(solution)/shard_map/all_to_all | solution.py:43
  17.9 0.1 reshape_squeeze.28
  18.0 0.1 reshape_squeeze.27
  18.1 1.1 convolution_convert_fusion.7
  19.2 13.0 %all-to-all-done = bf16[8,16,2048]{2,1,0:T(8,128)(2,1)S(1)} async-done(((bf16[8,16,2048]{2,1,0:T(8,128)(2,1)}), bf16[8,16,2048]{2,1,0:T(8,128)(2,1)S(1)}, u32[]{:S(2)}, u32[]{:S(2)}) %all-to-all-start) | async-done | bytes 524320 | tf_op jit(solution)/shard_map/all_to_all | solution.py:43
  32.1 4.4 all-to-all-start.1
  36.6 0.1 reduce_window_sum.27
  36.8 0.1 reshape_squeeze.30
  36.9 0.1 reduce_window_sum.32
  37.1 0.1 reshape_squeeze.29
  37.2 0.2 fusion.19
  37.4 1.1 convolution_convert_fusion.6
  38.4 12.5 %all-to-all-done.1 = bf16[8,16,2048]{2,1,0:T(8,128)(2,1)S(1)} async-done(((bf16[8,16,2048]{2,1,0:T(8,128)(2,1)}), bf16[8,16,2048]{2,1,0:T(8,128)(2,1)S(1)}, u32[]{:S(2)}, u32[]{:S(2)}) %all-to-all-start.1) | async-done | bytes 524320 | tf_op jit(solution)/shard_map/all_to_all | solution.py:43
  50.9 4.4 all-to-all-start.2
  55.3 0.1 reshape_squeeze.31
  55.4 1.1 convolution_convert_fusion.5
  56.5 13.2 %all-to-all-done.2 = bf16[8,16,2048]{2,1,0:T(8,128)(2,1)S(1)} async-done(((bf16[8,16,2048]{2,1,0:T(8,128)(2,1)}), bf16[8,16,2048]{2,1,0:T(8,128)(2,1)S(1)}, u32[]{:S(2)}, u32[]{:S(2)}) %all-to-all-start.2) | async-done | bytes 524320 | tf_op jit(solution)/shard_map/all_to_all | solution.py:43
  69.7 5.0 all-to-all-start.3
  74.7 3.1 bitcast_convert_fusion.3
  77.7 1.9 mul.122
  79.6 2.6 mul.123
  82.3 0.1 mul.120
  82.4 1.9 convolution_convert_fusion.3
  84.3 4.8 all-to-all-done.3
  89.2 4.5 all-to-all-start.4
  93.6 3.0 mul.127
  96.6 3.4 mul.128
  100.2 0.1 mul.125
  100.3 3.4 convolution_convert_fusion.2
  103.7 32.4 %all-to-all-done.4 = bf16[8,16,7168]{2,1,0:T(8,128)(2,1)S(1)} async-done(((bf16[8,16,7168]{2,1,0:T(8,128)(2,1)}), bf16[8,16,7168]{2,1,0:T(8,128)(2,1)S(1)}, u32[]{:S(2)}, u32[]{:S(2)}) %all-to-all-start.4) | async-done | bytes 1835040 | tf_op jit(solution)/shard_map/all_to_all | solution.py:50
  136.1 5.2 all-to-all-start.5
  141.3 3.0 mul.132
  144.3 3.4 mul.133
  147.8 0.1 mul.130
  147.9 3.5 convolution_convert_fusion.1
  151.4 32.4 %all-to-all-done.5 = bf16[8,16,7168]{2,1,0:T(8,128)(2,1)} async-done(((bf16[8,16,7168]{2,1,0:T(8,128)(2,1)}), bf16[8,16,7168]{2,1,0:T(8,128)(2,1)}, u32[]{:S(2)}, u32[]{:S(2)}) %all-to-all-start.5) | async-done | bytes 1835040 | tf_op jit(solution)/shard_map/all_to_all | solution.py:50
  183.8 5.2 all-to-all-start.6
  189.0 2.9 pad_maximum_fusion
  191.9 1.9 mul.137
  193.8 3.5 mul.138
  197.3 0.1 mul.135
  197.5 3.4 convolution_convert_fusion
  200.9 30.7 %all-to-all-done.6 = bf16[8,16,7168]{2,1,0:T(8,128)(2,1)} async-done(((bf16[8,16,7168]{2,1,0:T(8,128)(2,1)}), bf16[8,16,7168]{2,1,0:T(8,128)(2,1)}, u32[]{:S(2)}, u32[]{:S(2)}) %all-to-all-start.6) | async-done | bytes 1835040 | tf_op jit(solution)/shard_map/all_to_all | solution.py:50
  231.6 47.0 %all_to_all.55 = bf16[8,16,7168]{2,1,0:T(8,128)(2,1)S(1)} all-to-all(bf16[8,16,7168]{2,1,0:T(8,128)(2,1)} %bitcast.53), channel_id=1, replica_groups=mesh['rep'=4,'ep'=8] {'ep'}, dimensions={0} | all-to-all | bytes 3670016 | tf_op jit(solution)/shard_map/all_to_all | solution.py:50
  278.6 5.5 maximum_bitcast_fusion
  284.0 31.4 %copy.53 = bf16[1,512,7168]{1,0,2:T(2,128)(2,1)} copy(bf16[1,512,7168]{2,1,0:T(8,128)(2,1)} %maximum_bitcast_fusion) | data formatting | bytes 14680064 | tf_op jit(solution)/shard_map/reshape | solution.py:62
  315.5 0.5 broadcast.49
  316.0 48.2 %reduce = bf16[7168,512]{1,0:T(8,128)(2,1)} reduce(bf16[7168,1,512]{2,1,0:T(2,128)(2,1)} %bitcast.44, bf16[]{:T(256)} %broadcast.49), dimensions={1}, to_apply=%bitcast.36.reduce_sub_computation | reduce | bytes 14680066
  364.2 9.0 %reshape.177 = bf16[4,2,458752]{2,1,0:T(2,128)(2,1)} reshape(bf16[7168,512]{1,0:T(8,128)(2,1)} %reduce) | data formatting | bytes 14680064
  373.2 5.6 %all-to-all-start.8 = ((bf16[4,2,458752]{2,1,0:T(2,128)(2,1)}), bf16[4,2,458752]{2,1,0:T(2,128)(2,1)}, u32[]{:S(2)}, u32[]{:S(2)}) async-start(bf16[4,2,458752]{2,1,0:T(2,128)(2,1)} %reshape.177), calls=%async_computation.8 | async-start | bytes 14680064 | tf_op jit(solution)/shard_map/all_to_all | solution.py:63
  378.9 112.8 %psum.7 = f32[8]{0:T(128)S(1)} all-reduce(f32[8]{0:T(128)S(1)} %convert_add_fusion), channel_id=1, replica_groups=mesh['rep'=4,'ep'=8] {'rep','ep'}, use_global_device_ids=true, to_apply=%region_12.13 | all-reduce | flops 8 | bytes 64 | tf_op jit(solution)/shard_map/psum | solution.py:71
  491.7 0.5 broadcast_multiply_fusion
  492.2 11.3 %reshape.178 = bf16[7168,1,512]{2,1,0:T(2,128)(2,1)} reshape(bf16[4,2,458752]{2,1,0:T(2,128)(2,1)} %all-to-all-done.8) | data formatting | bytes 14680064
  503.5 10.4 %copy.55 = bf16[1,512,7168]{1,2,0:T(8,128)(2,1)} copy(bf16[1,512,7168]{1,0,2:T(2,128)(2,1)} %bitcast.45) | data formatting | bytes 14680064
  513.9 10.0 %copy.54 = bf16[4,1,512,1792]{3,2,0,1:T(8,128)(2,1)} copy(bf16[4,1,512,1792]{2,3,0,1:T(8,128)(2,1)} %bitcast.46) | data formatting | bytes 14680064 | tf_op jit(solution)/shard_map/all_to_all | solution.py:63
  523.9 21.2 %fusion = bf16[1,2048,1792]{2,1,0:T(8,128)(2,1)} fusion(bf16[2048,2048]{1,0:T(8,128)(2,1)} %all-gather.2.cloned.1.call-done, bf16[2048,1792]{1,0:T(8,128)(2,1)} %bitcast.49), kind=kOutput, calls=%fused_computation.6 | convolution fusion | flops 15036055552 | bytes 23068672 | tf_op jit(solution)/shard_map/dot_general | solution.py:65
  (29 shorter events, 1.2 us)
Async XLA Ops:
  12.2 19.9 %all-to-all-start = ((bf16[8,16,2048]{2,1,0:T(8,128)(2,1)}), bf16[8,16,2048]{2,1,0:T(8,128)(2,1)S(1)}, u32[]{:S(2)}, u32[]{:S(2)}) async-start(bf16[8,16,2048]{2,1,0:T(8,128)(2,1)} %bitcast), calls=%async_computation | async-start | bytes 1048576 | tf_op jit(solution)/shard_map/all_to_all | solution.py:43
  32.1 18.8 %all-to-all-start.1 = ((bf16[8,16,2048]{2,1,0:T(8,128)(2,1)}), bf16[8,16,2048]{2,1,0:T(8,128)(2,1)S(1)}, u32[]{:S(2)}, u32[]{:S(2)}) async-start(bf16[8,16,2048]{2,1,0:T(8,128)(2,1)} %bitcast.2), calls=%async_computation.1 | async-start | bytes 1048576 | tf_op jit(solution)/shard_map/all_to_all | solution.py:43
  50.9 26.8 %copy-start = (bf16[8,16,2048]{2,1,0:T(8,128)(2,1)}, bf16[8,16,2048]{2,1,0:T(8,128)(2,1)S(1)}, u32[]{:S(2)}) copy-start(bf16[8,16,2048]{2,1,0:T(8,128)(2,1)S(1)} %all-to-all-done.1) | copy-start | bytes 1572868
  50.9 18.8 %all-to-all-start.2 = ((bf16[8,16,2048]{2,1,0:T(8,128)(2,1)}), bf16[8,16,2048]{2,1,0:T(8,128)(2,1)S(1)}, u32[]{:S(2)}, u32[]{:S(2)}) async-start(bf16[8,16,2048]{2,1,0:T(8,128)(2,1)} %bitcast.4), calls=%async_computation.2 | async-start | bytes 1048576 | tf_op jit(solution)/shard_map/all_to_all | solution.py:43
  69.7 8.1 %copy-start.1 = (bf16[8,16,2048]{2,1,0:T(8,128)(2,1)}, bf16[8,16,2048]{2,1,0:T(8,128)(2,1)S(1)}, u32[]{:S(2)}) copy-start(bf16[8,16,2048]{2,1,0:T(8,128)(2,1)S(1)} %all-to-all-done.2) | copy-start | bytes 1572868
  69.7 19.5 %all-to-all-start.3 = ((bf16[8,16,2048]{2,1,0:T(8,128)(2,1)}), bf16[8,16,2048]{2,1,0:T(8,128)(2,1)}, u32[]{:S(2)}, u32[]{:S(2)}) async-start(bf16[8,16,2048]{2,1,0:T(8,128)(2,1)} %bitcast.6), calls=%async_computation.3 | async-start | bytes 1048576 | tf_op jit(solution)/shard_map/all_to_all | solution.py:43
  79.6 2.6 copy-start.2
  89.2 46.9 %all-to-all-start.4 = ((bf16[8,16,7168]{2,1,0:T(8,128)(2,1)}), bf16[8,16,7168]{2,1,0:T(8,128)(2,1)S(1)}, u32[]{:S(2)}, u32[]{:S(2)}) async-start(bf16[8,16,7168]{2,1,0:T(8,128)(2,1)} %bitcast.51), calls=%async_computation.4 | async-start | bytes 3670016 | tf_op jit(solution)/shard_map/all_to_all | solution.py:50
  136.1 47.7 %all-to-all-start.5 = ((bf16[8,16,7168]{2,1,0:T(8,128)(2,1)}), bf16[8,16,7168]{2,1,0:T(8,128)(2,1)}, u32[]{:S(2)}, u32[]{:S(2)}) async-start(bf16[8,16,7168]{2,1,0:T(8,128)(2,1)} %bitcast.52), calls=%async_computation.5 | async-start | bytes 3670016 | tf_op jit(solution)/shard_map/all_to_all | solution.py:50
  183.8 47.8 %all-to-all-start.6 = ((bf16[8,16,7168]{2,1,0:T(8,128)(2,1)}), bf16[8,16,7168]{2,1,0:T(8,128)(2,1)}, u32[]{:S(2)}, u32[]{:S(2)}) async-start(bf16[8,16,7168]{2,1,0:T(8,128)(2,1)} %bitcast.50), calls=%async_computation.6 | async-start | bytes 3670016 | tf_op jit(solution)/shard_map/all_to_all | solution.py:50
  189.0 334.9 %all-gather.2.cloned.1.call-start = ((), (), s32[]{:S(2)}) async-start(), calls=%async_computation.9 | async-start | bytes 10485760 | tf_op jit(solution)/shard_map/all_gather | solution.py:66
  373.2 118.9 %all-to-all-start.8 = ((bf16[4,2,458752]{2,1,0:T(2,128)(2,1)}), bf16[4,2,458752]{2,1,0:T(2,128)(2,1)}, u32[]{:S(2)}, u32[]{:S(2)}) async-start(bf16[4,2,458752]{2,1,0:T(2,128)(2,1)} %reshape.177), calls=%async_computation.8 | async-start | bytes 14680064 | tf_op jit(solution)/shard_map/all_to_all | solution.py:63
Sparse Core Ops, SparseCore 0:
  192.0 88.1 all-gather.1
where the time goes:
time: 557 us; the launch traced here: 552 us
  blocking collectives  160 us (29%)
  waiting for transfers between devices  139 us (25%)
  local copies, waits for them, and re-layouts  100 us (18%)
  other arithmetic  61.2 us (11%)
  starting transfers between devices  39.7 us (7%)
  matrix products  37.8 us (7%)
  between operations  14.2 us (3%)
    psum x1, blocking collectives, body(): all_loads = lax.psum(pair_loads, ('rep', 'ep'))  113 us
    all_to_all x3, waiting for transfers between devices, body(): lax.all_to_all(send_grad.reshape(owners, capacity, model_width), 'ep', sp...  95.5 us
    unnamed x1, other arithmetic  48.2 us
    all_to_all x1, blocking collectives, body(): lax.all_to_all(send_grad.reshape(owners, capacity, model_width), 'ep', sp...  47 us
    all_to_all x4, waiting for transfers between devices, body(): lax.all_to_all(send_hidden.reshape(owners, capacity, hidden_width), 'ep',...  43.5 us
    reshape x1, local copies, waits for them, and re-layouts, body(): jnp.concatenate(grad_stack, axis=0).reshape(1, all_rows, model_width)  31.4 us
    unnamed x10, local copies, waits for them, and re-layouts  31.3 us
    mul x12, local copies, waits for them, and re-layouts, body(): route_weight[micro_step][:, :, None]  23.1 us
  transfers between devices with their start and end apart: 9, of which 7 were waited for; matrix products, arithmetic and copies ran while one was open for 31% of the time, Pallas kernels for 0%

commit v1 on v0

--- a/solution.py
+++ b/solution.py
@@ -1,7 +1,324 @@
+import functools
+
 import jax
 import jax.numpy as jnp
 from jax import lax
+from jax.experimental import pallas as pl
+from jax.experimental.pallas import tpu as pltpu
 from jax.sharding import PartitionSpec as P
+
+MESH = pl.DeviceIdType.MESH
+CORES = 2
+VMEM_BYTES = 60 * 1024 * 1024
+
+
+def kernel(dims, send_ref, meta_ref, grad_ref, out_ref, load_ref, hid, met, gra, acc, picked, done,
+           sem_hs, sem_hf, sem_hr, sem_ms, sem_mf, sem_mr, sem_gs, sem_gr, sem_gup, sem_gdn, sem_gsib,
+           sem_gz, sem_gc, sem_loc, sem_out):
+    reps, owners, slots, tokens, width, columns, scale = dims
+    chips = owners // CORES
+    per_chip = reps * CORES
+    rep = lax.axis_index("rep")
+    own = lax.axis_index("ep")
+    z = own // CORES
+    core = lax.rem(own, CORES)
+    sib = z * CORES + (1 - core)
+
+    def place(r, e):
+        return (e // CORES) * per_chip + r * CORES + lax.rem(e, CORES)
+
+    def order(s):
+        low = jnp.minimum(z, chips - 1 - z)
+        near = s <= 2 * low
+        dist = jnp.where(near, (s + 1) // 2, s - low)
+        up = jnp.where(near, 1 - lax.rem(s, 2), jnp.where(z < chips - 1 - z, 1, 0))
+        sign = 2 * up - 1
+        return z + sign * dist, sign
+
+    def remote(src, dst, send, recv, **where):
+        return pltpu.make_async_remote_copy(
+            src_ref=src, dst_ref=dst, send_sem=send, recv_sem=recv,
+            device_id=where, device_id_type=MESH,
+        )
+
+    barrier = pltpu.get_barrier_semaphore()
+    for k in range(1, owners):
+        pl.semaphore_signal(barrier, inc=1, device_id={"ep": lax.rem(own + k, owners)}, device_id_type=MESH)
+    for k in range(1, reps):
+        pl.semaphore_signal(barrier, inc=1, device_id={"rep": lax.rem(rep + k, reps)}, device_id_type=MESH)
+    pl.semaphore_wait(barrier, owners - 1 + reps - 1)
+
+    here = place(rep, own)
+
+    def rows(e):
+        return send_ref.at[pl.ds(pl.multiple_of(e * slots, slots), slots)]
+
+    def slot_rows(i, n=1):
+        return hid.at[pl.ds(pl.multiple_of(i * slots, slots), n * slots)]
+
+    def cols(r):
+        return grad_ref.at[:, pl.ds(pl.multiple_of(r * columns, columns), columns)]
+
+    def dispatch(k):
+        e = lax.rem(own + k, owners)
+        return (
+            remote(meta_ref.at[e], met.at[here], sem_ms.at[k], sem_mr.at[here], ep=e),
+            remote(rows(e), slot_rows(here), sem_hs.at[k], sem_hr.at[here], ep=e),
+        )
+
+    def forward(e, k, first):
+        i = place(rep, e)
+        to = lax.rem(rep + k, reps)
+        m_src = meta_ref.at[own] if first else met.at[i]
+        h_src = rows(own) if first else slot_rows(i)
+        return (
+            remote(m_src, met.at[i], sem_mf.at[e, k], sem_mr.at[i], rep=to),
+            remote(h_src, slot_rows(i), sem_hf.at[e, k], sem_hr.at[i], rep=to),
+        )
+
+    def exchange(k):
+        to = lax.rem(rep + k, reps)
+        return remote(cols(to), gra.at[here], sem_gs.at[k], sem_gr.at[here], rep=to)
+
+    def g_src(i, first):
+        return cols(rep) if first else gra.at[i]
+
+    def g_up(i, first=False):
+        return remote(g_src(i, first), gra.at[i], sem_gup.at[i], sem_gz.at[i], ep=own + CORES)
+
+    def g_down(i, first=False):
+        return remote(g_src(i, first), gra.at[i], sem_gdn.at[i], sem_gz.at[i], ep=own - CORES)
+
+    def g_sib(i, first=False):
+        return remote(g_src(i, first), gra.at[i], sem_gsib.at[i], sem_gc.at[i], ep=sib)
+
+    def spread(i, first=False):
+        @pl.when(z < chips - 1)
+        def _():
+            g_up(i, first).start()
+
+        @pl.when(z > 0)
+        def _():
+            g_down(i, first).start()
+
+        g_sib(i, first).start()
+
+    local = (
+        pltpu.make_async_copy(meta_ref.at[own], met.at[here], sem_loc.at[0]),
+        pltpu.make_async_copy(rows(own), slot_rows(here), sem_loc.at[1]),
+        pltpu.make_async_copy(cols(rep), gra.at[here], sem_loc.at[2]),
+    )
+    for k in range(1, reps):
+        exchange(k).start()
+    for k in range(1, owners):
+        for c in dispatch(k):
+            c.start()
+    for c in local:
+        c.start()
+    for k in range(1, reps):
+        for c in forward(own, k, True):
+            c.start()
+    spread(here, True)
+
+    def pass_on(e):
+        i = place(rep, e)
+        remote(met.at[i], met.at[i], sem_ms.at[0], sem_mr.at[i], ep=own).wait_recv()
+        remote(slot_rows(i), slot_rows(i), sem_hs.at[0], sem_hr.at[i], ep=own).wait_recv()
+        for k in range(1, reps):
+            for c in forward(e, k, False):
+                c.start()
+
+    pass_on(sib)
+    for k in range(1, reps):
+        i = place(lax.rem(rep + k, reps), own)
+        remote(gra.at[i], gra.at[i], sem_gs.at[0], sem_gr.at[i], ep=own).wait_recv()
+        spread(i)
+
+    def pass_chip(s, carry):
+        chip, _ = order(s)
+        for c in range(CORES):
+            pass_on(chip * CORES + c)
+        return carry
+
+    lax.fori_loop(1, chips, pass_chip, 0)
+    for c in local:
+        c.wait()
+
+    half = reps // 2
+    group = half * CORES
+    depth = group * slots
+    tile = 256
+
+    def step(s, first, last):
+        chip, sign = order(s)
+        for part in range(2):
+            for j in range(half):
+                r = part * half + j
+                mine = chip * per_chip + r * CORES + core
+                other = chip * per_chip + r * CORES + (1 - core)
+                if not first:
+                    remote(gra.at[mine], gra.at[mine], sem_gs.at[0], sem_gz.at[mine], ep=own).wait_recv()
+
+                    @pl.when((sign < 0) & (z < chips - 1))
+                    def _():
+                        g_up(mine).start()
+
+                    @pl.when((sign > 0) & (z > 0))
+                    def _():
+                        g_down(mine).start()
+
+                    g_sib(mine).start()
+            for j in range(half):
+                r = part * half + j
+                other = chip * per_chip + r * CORES + (1 - core)
+                remote(gra.at[other], gra.at[other], sem_gs.at[0], sem_gc.at[other], ep=own).wait_recv()
+
+                @pl.when(r != rep)
+                def _():
+                    for c in range(CORES):
+                        i = chip * per_chip + r * CORES + c
+                        remote(met.at[i], met.at[i], sem_ms.at[0], sem_mr.at[i], ep=own).wait_recv()
+                        remote(slot_rows(i), slot_rows(i), sem_hs.at[0], sem_hr.at[i], ep=own).wait_recv()
+
+            base = chip * per_chip + part * group
+
+            def select(g, carry):
+                info = met[base + g]
+                row = lax.broadcasted_iota(jnp.int32, (slots, tokens), 0).astype(jnp.float32)
+                hit = row == info[0:1, :]
+                weight = jnp.sum(jnp.where(hit, info[1:2, :], 0.0), axis=1, keepdims=True)
+                rows_g = jnp.dot(hit.astype(jnp.bfloat16), gra[base + g], preferred_element_type=jnp.float32)
+                picked[pl.ds(pl.multiple_of(g * slots, slots), slots), :] = (weight * rows_g).astype(jnp.bfloat16)
+                return carry
+
+            lax.fori_loop(0, group, select, 0)
+
+            def block(t, carry):
+                at = pl.ds(pl.multiple_of(t * tile, tile), tile)
+                lhs = hid[pl.ds(pl.multiple_of(base * slots, slots), depth), at]
+                prod = lax.dot_general(lhs, picked[...], (((0,), (0,)), ((), ())), preferred_element_type=jnp.float32)
+                if first and part == 0:
+                    acc[at, :] = prod
+                elif last and part == 1:
+                    done[at, :] = (acc[at, :] + prod).astype(jnp.bfloat16)
+                    pltpu.make_async_copy(done.at[at], out_ref.at[at], sem_out.at[t]).start()
+                else:
+                    acc[at, :] += prod
+                return carry
+
+            lax.fori_loop(0, width // tile, block, 0)
+
+    step(0, True, chips == 1)
+
+    def middle(s, carry):
+        step(s, False, False)
+        return carry
+
+    lax.fori_loop(1, chips - 1, middle, 0)
+    step(chips - 1, False, True)
+
+    load_ref[...] = jnp.sum(met[...], axis=0) * scale
+
+    for k in range(1, reps):
+        exchange(k).wait_send()
+    for k in range(1, owners):
+        for c in dispatch(k):
+            c.wait_send()
+
+    def drain(e, carry):
+        for k in range(1, reps):
+            i = place(rep, e)
+            to = lax.rem(rep + k, reps)
+            remote(met.at[i], met.at[i], sem_mf.at[e, k], sem_mr.at[i], rep=to).wait_send()
+            remote(slot_rows(i), slot_rows(i), sem_hf.at[e, k], sem_hr.at[i], rep=to).wait_send()
+        chip = e // CORES
+
+        @pl.when(lax.rem(e, CORES) == core)
+        def _():
+            for r in range(reps):
+                i = chip * per_chip + r * CORES + core
+                g_sib(i).wait_send()
+
+                @pl.when((chip <= z) & (z < chips - 1))
+                def _():
+                    g_up(i).wait_send()
+
+                @pl.when((chip >= z) & (z > 0))
+                def _():
+                    g_down(i).wait_send()
+
+        return carry
+
+    lax.fori_loop(0, owners, drain, 0)
+
+    def flush(t, carry):
+        at = pl.ds(pl.multiple_of(t * tile, tile), tile)
+        pltpu.make_async_copy(done.at[at], out_ref.at[at], sem_out.at[t]).wait()
+        return carry
+
+    lax.fori_loop(0, width // tile, flush, 0)
+
+
+def fused(hidden, out_grad, route_weight, expert_ids):
+    micro_count, tokens_here, choices_per, hidden_width = hidden.shape
+    model_width = out_grad.shape[2]
+    replicas = lax.axis_size("rep")
+    owners = lax.axis_size("ep")
+    capacity = 2 * tokens_here * choices_per // owners
+    columns = model_width // replicas
+    pair_count = tokens_here * choices_per
+    tokens = micro_count * tokens_here
+    slots = micro_count * capacity
+    devices = replicas * owners
+    total = micro_count * tokens_here * devices * choices_per
+
+    ids = expert_ids.reshape(micro_count, pair_count)
+    expert_index = jnp.arange(owners, dtype=jnp.int32)
+    matches = ids[:, :, None] == expert_index
+    ones = matches.astype(jnp.bfloat16)
+    before = (jnp.arange(pair_count)[:, None] > jnp.arange(pair_count)[None, :]).astype(jnp.bfloat16)
+    earlier = jnp.einsum("pq,mqe->mpe", before, ones, preferred_element_type=jnp.float32)
+    spot = earlier + (capacity * jnp.arange(micro_count, dtype=jnp.float32))[:, None, None]
+    in_expert = jnp.sum(jnp.where(matches, spot, 0.0), axis=2)
+    slot_of_pair = (ids * slots + in_expert.astype(jnp.int32)).reshape(micro_count * pair_count)
+    selector = (jnp.arange(owners * slots, dtype=jnp.int32)[:, None] == slot_of_pair[None, :]).astype(jnp.bfloat16)
+    send_hidden = jnp.dot(
+        selector, hidden.reshape(micro_count * pair_count, hidden_width), preferred_element_type=jnp.float32
+    ).astype(jnp.bfloat16)
+    by_token = matches.reshape(tokens, choices_per, owners)
+    spot_row = jnp.max(jnp.where(by_token, spot.reshape(tokens, choices_per, owners), -1.0), axis=1).T
+    weight_row = jnp.sum(jnp.where(by_token, route_weight.reshape(tokens, choices_per, 1), 0.0), axis=1).T
+    counts = jnp.sum(by_token.astype(jnp.float32), axis=(0, 1))
+    count_row = jnp.broadcast_to(jnp.pad(counts, (0, tokens - owners))[None, :], (owners, tokens))
+    meta = jnp.stack([spot_row, weight_row, count_row] + [jnp.zeros_like(spot_row)] * 5, axis=1)
+
+    dims = (replicas, owners, slots, tokens, hidden_width, columns, owners / total)
+    dma = pltpu.SemaphoreType.DMA
+    result, load = pl.pallas_call(
+        functools.partial(kernel, dims),
+        out_shape=(
+            jax.ShapeDtypeStruct((hidden_width, columns), jnp.bfloat16),
+            jax.ShapeDtypeStruct((8, tokens), jnp.float32),
+        ),
+        in_specs=[pl.BlockSpec(memory_space=pl.ANY)] * 3,
+        out_specs=(pl.BlockSpec(memory_space=pl.ANY), pl.BlockSpec(memory_space=pltpu.VMEM)),
+        scratch_shapes=[
+            pltpu.VMEM((devices * slots, hidden_width), jnp.bfloat16),
+            pltpu.VMEM((devices, 8, tokens), jnp.float32),
+            pltpu.VMEM((devices, tokens, columns), jnp.bfloat16),
+            pltpu.VMEM((hidden_width, columns), jnp.float32),
+            pltpu.VMEM((replicas // 2 * CORES * slots, columns), jnp.bfloat16),
+            pltpu.VMEM((hidden_width, columns), jnp.bfloat16),
+            dma((owners,)), dma((owners, replicas)), dma((devices,)),
+            dma((owners,)), dma((owners, replicas)), dma((devices,)),
+            dma((replicas,)), dma((devices,)), dma((devices,)), dma((devices,)), dma((devices,)),
+            dma((devices,)), dma((devices,)), dma((3,)), dma((hidden_width // 256,)),
+        ],
+        compiler_params=pltpu.CompilerParams(
+            collective_id=0, has_side_effects=True, vmem_limit_bytes=VMEM_BYTES
+        ),
+    )(send_hidden, meta, out_grad.reshape(tokens, model_width))
+    return result.reshape(1, hidden_width, columns), load[2, :owners]
 
 
 def body(hidden, out_grad, route_weight, expert_ids):
@@ -74,8 +391,17 @@
 
 
 def solution(mesh):
+    def plan(hidden, out_grad, route_weight, expert_ids):
+        devices = mesh.shape["rep"] * mesh.shape["ep"]
+        tokens = hidden.shape[0] * hidden.shape[1]
+        columns = out_grad.shape[2] // mesh.shape["rep"]
+        slots = 2 * tokens * hidden.shape[2] // mesh.shape["ep"]
+        held = 2 * devices * (tokens * columns + slots * hidden.shape[3]) + 6 * hidden.shape[3] * columns
+        run = fused if held < 0.85 * VMEM_BYTES else body
+        return run(hidden, out_grad, route_weight, expert_ids)
+
     return jax.shard_map(
-        body,
+        plan,
         mesh=mesh,
         in_specs=(
             P(None, ("rep", "ep"), None, None),

time: 557 us -> 202 us (0.36)
  Pallas kernels: 0 us -> 184 us
  blocking collectives: 160 us -> 0 us
  waiting for transfers between devices: 139 us -> 0 us
  local copies, waits for them, and re-layouts: 100 us -> 12.9 us
  other arithmetic: 61.2 us -> 1.21 us
  starting transfers between devices: 39.7 us -> 0 us
  matrix products: 37.8 us -> 2.2 us
  between operations: 14.2 us -> 0.71 us
    pallas_call x0 -> x1, Pallas kernels: none -> 184 us  [fused(): pl.pallas_call(functools.partial(kernel, dims), out_shape=(jax.ShapeDtype...]
    all_to_all x8 -> x0, waiting for transfers between devices: 139 us -> none  [the longest x3 95.5 us: body(): lax.all_to_all(send_grad.reshape(owners, capacity, model_width), 'ep', sp...]
    psum x1 -> x0, blocking collectives: 113 us -> none  [body(): all_loads = lax.psum(pair_loads, ('rep', 'ep'))]
    unnamed x1 -> x0, other arithmetic: 48.2 us -> none
    all_to_all x1 -> x0, blocking collectives: 47 us -> none  [body(): lax.all_to_all(send_grad.reshape(owners, capacity, model_width), 'ep', sp...]
    all_to_all x8 -> x0, starting transfers between devices: 39.7 us -> none  [the longest x4 19.3 us: body(): lax.all_to_all(send_hidden.reshape(owners, capacity, hidden_width), 'ep',...]
    dot_general x9 -> x2, matrix products: 37.8 us -> 2.2 us  [the longest x1 2.04 us: fused(): jnp.dot(selector, hidden.reshape(micro_count * pair_count, hidden_width),...]
    reshape x1, local copies, waits for them, and re-layouts: 31.4 us -> 1.46 us  [fused(): hidden.reshape(micro_count * pair_count, hidden_width)]
  transfers between devices with their start and end apart: 9 -> 0, of which waited for: 7 -> 0; matrix products, arithmetic and copies ran while one was open for 31% -> 0% of each run, Pallas kernels for 0% -> 0%
where the time goes in v1:
time: 202 us; the launch traced here: 201 us
  Pallas kernels  184 us (91%)
  local copies, waits for them, and re-layouts  12.9 us (6%)
  matrix products  2.2 us (1%)
    pallas_call x1, Pallas kernels, fused(): pl.pallas_call(functools.partial(kernel, dims), out_shape=(jax.ShapeDtype...  184 us
    unnamed x2, local copies, waits for them, and re-layouts  7.38 us

profile of v1, /device:TPU:3, one launch (start us, length us, event | category | flops | bytes accessed | tf_op | source)
XLA Modules:
  0.0 201.2 jit_solution(4099645354321913168)
XLA Ops:
  0.6 0.7 broadcast_multiply_fusion
  1.3 0.8 copy.15
  2.1 0.1 copy.16
  2.2 0.2 select_reduce_fusion.2
  2.4 0.1 convert_element_type.22
  2.4 0.1 copy.14
  2.6 0.1 mul.22
  2.7 0.8 copy.25
  3.5 0.8 copy.24
  4.3 0.1 copy.19
  4.4 0.5 convert_reduce_fusion
  5.0 0.1 copy.20
  5.0 0.7 stack.15.meta_ref
  5.7 1.5 reshape.41
  7.2 2.0 %convolution_convert_fusion.send_ref = bf16[512,2048]{1,0:T(8,128)(2,1)} fusion(bf16[256,2048]{1,0:T(8,128)(2,1)S(1)} %reshape.41, s32[256]{0:T(256)S(1)} %add.23), kind=kOutput, calls=%fused_computation | convolution fusion | flops 538050560 | bytes 3146752 | tf_op jit(solution)/shard_map/dot_general | solution.py:285
  9.2 184.2 %shard_map.59 = (bf16[2048,1792]{1,0:T(8,128)(2,1)}, f32[8,128]{1,0:T(8,128)}) custom-call(bf16[512,2048]{1,0:T(8,128)(2,1)} %convolution_convert_fusion.send_ref, f32[8,8,128]{2,1,0:T(8,128)} %stack.15.meta_ref, bf16[128,7168]{1,0:T(8,128)(2,1)} %bitcast.23), custom_call_target="tpu_custom_call" | custom-call | tf_op jit(solution)/shard_map/pallas_call | solution.py:297
  193.4 1.2 slice_bitcast_fusion
  194.6 6.6 %copy.29 = bf16[1,2048,1792]{2,1,0:T(8,128)(2,1)} copy(bf16[1,2048,1792]{2,1,0:T(8,128)(2,1)} %bitcast.22) | data formatting | bytes 14680064
  (8 shorter events, 0.1 us)

commit v2 on v1

--- a/solution.py
+++ b/solution.py
@@ -9,13 +9,14 @@
 
 MESH = pl.DeviceIdType.MESH
 CORES = 2
-VMEM_BYTES = 60 * 1024 * 1024
-
-
-def kernel(dims, send_ref, meta_ref, grad_ref, out_ref, load_ref, hid, met, gra, acc, picked, done,
+VMEM_BYTES = 52 * 1024 * 1024
+KERNEL_BYTES = 44 * 1024 * 1024
+
+
+def kernel(dims, aux_ref, hidden_ref, grad_ref, out_ref, load_ref, hid, met, gra, acc, picked, packed, table,
            sem_hs, sem_hf, sem_hr, sem_ms, sem_mf, sem_mr, sem_gs, sem_gr, sem_gup, sem_gdn, sem_gsib,
-           sem_gz, sem_gc, sem_loc, sem_out):
-    reps, owners, slots, tokens, width, columns, scale = dims
+           sem_gz, sem_gc, sem_loc):
+    reps, owners, slots, tokens, width, columns, micro, scale = dims
     chips = owners // CORES
     per_chip = reps * CORES
     rep = lax.axis_index("rep")
@@ -51,7 +52,7 @@
     here = place(rep, own)
 
     def rows(e):
-        return send_ref.at[pl.ds(pl.multiple_of(e * slots, slots), slots)]
+        return packed.at[pl.ds(pl.multiple_of(e * slots, slots), slots)]
 
     def slot_rows(i, n=1):
         return hid.at[pl.ds(pl.multiple_of(i * slots, slots), n * slots)]
@@ -62,18 +63,16 @@
     def dispatch(k):
         e = lax.rem(own + k, owners)
         return (
-            remote(meta_ref.at[e], met.at[here], sem_ms.at[k], sem_mr.at[here], ep=e),
+            remote(table.at[e], met.at[here], sem_ms.at[k], sem_mr.at[here], ep=e),
             remote(rows(e), slot_rows(here), sem_hs.at[k], sem_hr.at[here], ep=e),
         )
 
-    def forward(e, k, first):
+    def forward(e, k):
         i = place(rep, e)
         to = lax.rem(rep + k, reps)
-        m_src = meta_ref.at[own] if first else met.at[i]
-        h_src = rows(own) if first else slot_rows(i)
         return (
-            remote(m_src, met.at[i], sem_mf.at[e, k], sem_mr.at[i], rep=to),
-            remote(h_src, slot_rows(i), sem_hf.at[e, k], sem_hr.at[i], rep=to),
+            remote(met.at[i], met.at[i], sem_mf.at[e, k], sem_mr.at[i], rep=to),
+            remote(slot_rows(i), slot_rows(i), sem_hf.at[e, k], sem_hr.at[i], rep=to),
         )
 
     def exchange(k):
@@ -103,29 +102,72 @@
 
         g_sib(i, first).start()
 
-    local = (
-        pltpu.make_async_copy(meta_ref.at[own], met.at[here], sem_loc.at[0]),
-        pltpu.make_async_copy(rows(own), slot_rows(here), sem_loc.at[1]),
-        pltpu.make_async_copy(cols(rep), gra.at[here], sem_loc.at[2]),
-    )
+    local = pltpu.make_async_copy(cols(rep), gra.at[here], sem_loc.at[0])
     for k in range(1, reps):
         exchange(k).start()
-    for k in range(1, owners):
-        for c in dispatch(k):
+    spread(here, True)
+    local.start()
+
+    ids = [aux_ref[k : k + 1, :] for k in range(2)]
+    weights = [aux_ref[2 + k : 3 + k, :] for k in range(2)]
+    expert = lax.broadcasted_iota(jnp.int32, (owners, tokens), 0).astype(jnp.float32)
+    match = [expert == ids[k] for k in range(2)]
+    taken = jnp.where(match[0] | match[1], 1.0, 0.0)
+    before = lax.broadcasted_iota(jnp.int32, (tokens, tokens), 0)
+    after = lax.broadcasted_iota(jnp.int32, (tokens, tokens), 1)
+    per_micro = tokens // micro
+    same = lax.div(before, per_micro) == lax.div(after, per_micro)
+    tri = jnp.where(same & (before < after), 1.0, 0.0).astype(jnp.bfloat16)
+    earlier = jnp.dot(taken.astype(jnp.bfloat16), tri, preferred_element_type=jnp.float32)
+    step_of = lax.div(lax.broadcasted_iota(jnp.int32, (owners, tokens), 1), per_micro)
+    spot = jnp.where(taken > 0.0, earlier + (step_of * (slots // micro)).astype(jnp.float32), -1.0)
+    weight_of = jnp.where(match[0], weights[0], jnp.where(match[1], weights[1], 0.0))
+    counts = jnp.broadcast_to(jnp.sum(taken, axis=1, keepdims=True), (owners, tokens))
+    for e in range(owners):
+        first_choice = jnp.where(match[0][e : e + 1, :], 1.0, 0.0)
+        table[e, 0:1, :] = spot[e : e + 1, :]
+        table[e, 1:2, :] = weight_of[e : e + 1, :]
+        table[e, 2:3, :] = first_choice
+        table[e, 3:8, :] = jnp.zeros((5, tokens), jnp.float32)
+        table[e, 8:, :] = counts
+
+    def pack(e):
+        info = table[e]
+        row = lax.broadcasted_iota(jnp.int32, (slots, tokens), 0).astype(jnp.float32)
+        hit = row == info[0:1, :]
+        one = hit & (info[2:3, :] > 0.0)
+        two = hit & (info[2:3, :] == 0.0)
+        both = jnp.dot(one.astype(jnp.bfloat16), hidden_ref[:, :width], preferred_element_type=jnp.float32)
+        both += jnp.dot(two.astype(jnp.bfloat16), hidden_ref[:, width:], preferred_element_type=jnp.float32)
+        return both.astype(jnp.bfloat16)
+
+    hid[pl.ds(pl.multiple_of(here * slots, slots), slots), :] = pack(own)
+    met[here] = table[own]
+
+    def pack_and_send(k, carry):
+        e = lax.rem(own + k, owners)
+        packed[pl.ds(pl.multiple_of(e * slots, slots), slots), :] = pack(e)
+
+        @pl.when(k > 1)
+        def _():
+            for c in dispatch(k - 1):
+                c.start()
+
+        return carry
+
+    lax.fori_loop(1, owners, pack_and_send, 0)
+    for k in range(1, reps):
+        for c in forward(own, k):
             c.start()
-    for c in local:
+    for c in dispatch(owners - 1):
         c.start()
-    for k in range(1, reps):
-        for c in forward(own, k, True):
-            c.start()
-    spread(here, True)
 
     def pass_on(e):
         i = place(rep, e)
         remote(met.at[i], met.at[i], sem_ms.at[0], sem_mr.at[i], ep=own).wait_recv()
         remote(slot_rows(i), slot_rows(i), sem_hs.at[0], sem_hr.at[i], ep=own).wait_recv()
         for k in range(1, reps):
-            for c in forward(e, k, False):
+            for c in forward(e, k):
                 c.start()
 
     pass_on(sib)
@@ -141,21 +183,21 @@
         return carry
 
     lax.fori_loop(1, chips, pass_chip, 0)
-    for c in local:
-        c.wait()
+    local.wait()
 
     half = reps // 2
-    group = half * CORES
-    depth = group * slots
     tile = 256
 
     def step(s, first, last):
         chip, sign = order(s)
-        for part in range(2):
-            for j in range(half):
-                r = part * half + j
+        parts = [(0, half), (half, half)]
+        if last:
+            parts = [(0, half)] + [(r, 1) for r in range(half, reps)]
+        for start, count in parts:
+            group = count * CORES
+            depth = group * slots
+            for r in range(start, start + count):
                 mine = chip * per_chip + r * CORES + core
-                other = chip * per_chip + r * CORES + (1 - core)
                 if not first:
                     remote(gra.at[mine], gra.at[mine], sem_gs.at[0], sem_gz.at[mine], ep=own).wait_recv()
 
@@ -168,8 +210,7 @@
                         g_down(mine).start()
 
                     g_sib(mine).start()
-            for j in range(half):
-                r = part * half + j
+            for r in range(start, start + count):
                 other = chip * per_chip + r * CORES + (1 - core)
                 remote(gra.at[other], gra.at[other], sem_gs.at[0], sem_gc.at[other], ep=own).wait_recv()
 
@@ -180,7 +221,7 @@
                         remote(met.at[i], met.at[i], sem_ms.at[0], sem_mr.at[i], ep=own).wait_recv()
                         remote(slot_rows(i), slot_rows(i), sem_hs.at[0], sem_hr.at[i], ep=own).wait_recv()
 
-            base = chip * per_chip + part * group
+            base = chip * per_chip + start * CORES
 
             def select(g, carry):
                 info = met[base + g]
@@ -196,12 +237,11 @@
             def block(t, carry):
                 at = pl.ds(pl.multiple_of(t * tile, tile), tile)
                 lhs = hid[pl.ds(pl.multiple_of(base * slots, slots), depth), at]
-                prod = lax.dot_general(lhs, picked[...], (((0,), (0,)), ((), ())), preferred_element_type=jnp.float32)
-                if first and part == 0:
+                prod = lax.dot_general(lhs, picked[:depth, :], (((0,), (0,)), ((), ())), preferred_element_type=jnp.float32)
+                if first and start == 0:
                     acc[at, :] = prod
-                elif last and part == 1:
-                    done[at, :] = (acc[at, :] + prod).astype(jnp.bfloat16)
-                    pltpu.make_async_copy(done.at[at], out_ref.at[at], sem_out.at[t]).start()
+                elif last and start + count == reps:
+                    out_ref[at, :] = (acc[at, :] + prod).astype(jnp.bfloat16)
                 else:
                     acc[at, :] += prod
                 return carry
@@ -217,7 +257,7 @@
     lax.fori_loop(1, chips - 1, middle, 0)
     step(chips - 1, False, True)
 
-    load_ref[...] = jnp.sum(met[...], axis=0) * scale
+    load_ref[...] = jnp.sum(met[:, 8:, :], axis=0) * scale
 
     for k in range(1, reps):
         exchange(k).wait_send()
@@ -251,13 +291,6 @@
 
     lax.fori_loop(0, owners, drain, 0)
 
-    def flush(t, carry):
-        at = pl.ds(pl.multiple_of(t * tile, tile), tile)
-        pltpu.make_async_copy(done.at[at], out_ref.at[at], sem_out.at[t]).wait()
-        return carry
-
-    lax.fori_loop(0, width // tile, flush, 0)
-
 
 def fused(hidden, out_grad, route_weight, expert_ids):
     micro_count, tokens_here, choices_per, hidden_width = hidden.shape
@@ -266,59 +299,47 @@
     owners = lax.axis_size("ep")
     capacity = 2 * tokens_here * choices_per // owners
     columns = model_width // replicas
-    pair_count = tokens_here * choices_per
     tokens = micro_count * tokens_here
     slots = micro_count * capacity
     devices = replicas * owners
     total = micro_count * tokens_here * devices * choices_per
 
-    ids = expert_ids.reshape(micro_count, pair_count)
-    expert_index = jnp.arange(owners, dtype=jnp.int32)
-    matches = ids[:, :, None] == expert_index
-    ones = matches.astype(jnp.bfloat16)
-    before = (jnp.arange(pair_count)[:, None] > jnp.arange(pair_count)[None, :]).astype(jnp.bfloat16)
-    earlier = jnp.einsum("pq,mqe->mpe", before, ones, preferred_element_type=jnp.float32)
-    spot = earlier + (capacity * jnp.arange(micro_count, dtype=jnp.float32))[:, None, None]
-    in_expert = jnp.sum(jnp.where(matches, spot, 0.0), axis=2)
-    slot_of_pair = (ids * slots + in_expert.astype(jnp.int32)).reshape(micro_count * pair_count)
-    selector = (jnp.arange(owners * slots, dtype=jnp.int32)[:, None] == slot_of_pair[None, :]).astype(jnp.bfloat16)
-    send_hidden = jnp.dot(
-        selector, hidden.reshape(micro_count * pair_count, hidden_width), preferred_element_type=jnp.float32
-    ).astype(jnp.bfloat16)
-    by_token = matches.reshape(tokens, choices_per, owners)
-    spot_row = jnp.max(jnp.where(by_token, spot.reshape(tokens, choices_per, owners), -1.0), axis=1).T
-    weight_row = jnp.sum(jnp.where(by_token, route_weight.reshape(tokens, choices_per, 1), 0.0), axis=1).T
-    counts = jnp.sum(by_token.astype(jnp.float32), axis=(0, 1))
-    count_row = jnp.broadcast_to(jnp.pad(counts, (0, tokens - owners))[None, :], (owners, tokens))
-    meta = jnp.stack([spot_row, weight_row, count_row] + [jnp.zeros_like(spot_row)] * 5, axis=1)
-
-    dims = (replicas, owners, slots, tokens, hidden_width, columns, owners / total)
+    routes = jnp.concatenate(
+        [
+            expert_ids.reshape(tokens, choices_per).T.astype(jnp.float32),
+            route_weight.reshape(tokens, choices_per).T,
+        ],
+        axis=0,
+    )
+
+    dims = (replicas, owners, slots, tokens, hidden_width, columns, micro_count, owners / total)
     dma = pltpu.SemaphoreType.DMA
     result, load = pl.pallas_call(
         functools.partial(kernel, dims),
         out_shape=(
             jax.ShapeDtypeStruct((hidden_width, columns), jnp.bfloat16),
-            jax.ShapeDtypeStruct((8, tokens), jnp.float32),
+            jax.ShapeDtypeStruct((owners, tokens), jnp.float32),
         ),
-        in_specs=[pl.BlockSpec(memory_space=pl.ANY)] * 3,
-        out_specs=(pl.BlockSpec(memory_space=pl.ANY), pl.BlockSpec(memory_space=pltpu.VMEM)),
+        in_specs=[pl.BlockSpec(memory_space=pltpu.VMEM)] * 2 + [pl.BlockSpec(memory_space=pl.ANY)],
+        out_specs=(pl.BlockSpec(memory_space=pltpu.VMEM),) * 2,
         scratch_shapes=[
             pltpu.VMEM((devices * slots, hidden_width), jnp.bfloat16),
-            pltpu.VMEM((devices, 8, tokens), jnp.float32),
+            pltpu.VMEM((devices, 8 + owners, tokens), jnp.float32),
             pltpu.VMEM((devices, tokens, columns), jnp.bfloat16),
             pltpu.VMEM((hidden_width, columns), jnp.float32),
             pltpu.VMEM((replicas // 2 * CORES * slots, columns), jnp.bfloat16),
-            pltpu.VMEM((hidden_width, columns), jnp.bfloat16),
+            pltpu.VMEM((owners * slots, hidden_width), jnp.bfloat16),
+            pltpu.VMEM((owners, 8 + owners, tokens), jnp.float32),
             dma((owners,)), dma((owners, replicas)), dma((devices,)),
             dma((owners,)), dma((owners, replicas)), dma((devices,)),
             dma((replicas,)), dma((devices,)), dma((devices,)), dma((devices,)), dma((devices,)),
-            dma((devices,)), dma((devices,)), dma((3,)), dma((hidden_width // 256,)),
+            dma((devices,)), dma((devices,)), dma((1,)),
         ],
         compiler_params=pltpu.CompilerParams(
-            collective_id=0, has_side_effects=True, vmem_limit_bytes=VMEM_BYTES
+            collective_id=0, has_side_effects=True, vmem_limit_bytes=KERNEL_BYTES
         ),
-    )(send_hidden, meta, out_grad.reshape(tokens, model_width))
-    return result.reshape(1, hidden_width, columns), load[2, :owners]
+    )(routes, hidden.reshape(tokens, choices_per * hidden_width), out_grad.reshape(tokens, model_width))
+    return result.reshape(1, hidden_width, columns), load[:, 0]
 
 
 def body(hidden, out_grad, route_weight, expert_ids):
@@ -397,7 +418,7 @@
         columns = out_grad.shape[2] // mesh.shape["rep"]
         slots = 2 * tokens * hidden.shape[2] // mesh.shape["ep"]
         held = 2 * devices * (tokens * columns + slots * hidden.shape[3]) + 6 * hidden.shape[3] * columns
-        run = fused if held < 0.85 * VMEM_BYTES else body
+        run = fused if held < 0.9 * VMEM_BYTES else body
         return run(hidden, out_grad, route_weight, expert_ids)
 
     return jax.shard_map(

time: 202 us -> 192 us (0.950)
  local copies, waits for them, and re-layouts: 12.9 us -> 7.62 us
  matrix products: 2.2 us -> 0 us
    dot_general x2 -> x0, matrix products: 2.2 us -> none  [the longest x1 2.04 us: fused(): jnp.dot(selector, hidden.reshape(micro_count * pair_count, hidden_width),...]
    unnamed x2 -> x5, local copies, waits for them, and re-layouts: 7.38 us -> 6.82 us
where the time goes in v2:
time: 192 us
  Pallas kernels  183 us (95%)
  local copies, waits for them, and re-layouts  7.62 us (4%)
    pallas_call x1, Pallas kernels, fused(): pl.pallas_call(functools.partial(kernel, dims), out_shape=(jax.ShapeDtype...  183 us
    unnamed x5, local copies, waits for them, and re-layouts  6.82 us

profile of v2, /device:TPU:3, one launch (start us, length us, event | category | flops | bytes accessed | tf_op | source)
XLA Modules:
  0.0 191.6 jit_solution(992126472654320908)
XLA Ops:
  0.6 0.7 copy.9
  1.3 0.1 reshape.18
  1.4 0.7 convert_element_type.9
  2.1 0.1 convert_element_type.10
  2.2 1.6 copy.10
  3.8 0.0 copy-start
  3.8 1.5 copy-done
  5.3 182.6 %shard_map.59 = (bf16[2048,1792]{1,0:T(8,128)(2,1)S(1)}, f32[8,128]{1,0:T(8,128)S(1)}) custom-call(f32[4,128]{1,0:T(4,128)S(1)} %pad_maximum_fusion.aux_ref, bf16[128,4096]{1,0:T(8,128)(2,1)S(1)} %bitcast.12, bf16[128,7168]{1,0:T(8,128)(2,1)S(1)} %bitcast.13), custom_call_target="tpu_custom_call" | custom-call | tf_op jit(solution)/shard_map/pallas_call | solution.py:317
  187.9 0.6 slice_reduce_fusion
  188.6 3.0 %copy.12 = bf16[1,2048,1792]{2,1,0:T(8,128)(2,1)} copy(bf16[1,2048,1792]{2,1,0:T(8,128)(2,1)S(1)} %bitcast.11) | data formatting | bytes 14680064
  (2 shorter events, 0.0 us)
Async XLA Ops:
  3.8 1.5 copy-start
